TPU v7x, 32 devices: a whole 2x2x4 slice. The times are simulated.
32 devices in a mesh: section: 2 (over x), dp: 16 (over z, y, core).
Axes of the slice: x: 2, y: 2, z: 4, core: 2. Of those that a mesh axis runs over, the one named last changes fastest.
Arguments:
- activations: bfloat16 [2, 8, 768, 5376], P('section', None, 'dp'), may hold values from -6 to 6
- loss_grads: bfloat16 [8, 768, 5376], P(None, 'dp'), may hold values from -6 to 6
- adapter_in: bfloat16 [2, 5376, 64], P('section'), may hold values from -0.078125 to 0.078125
- adapter_out: bfloat16 [2, 64, 5376], P('section'), may hold values from -0.75 to 0.75
- first_moment: float32 [2, 16, 86016], P('section', 'dp'), may hold values from -0.4 to 0.4
- second_moment: float32 [2, 16, 86016], P('section', 'dp'), may hold values from 0.0001 to 0.01
- old_owner: int32 [2, 8], P('section'), may hold values from 0 to 15, as said below
- new_owner: int32 [2, 16], P('section'), may hold values from 0 to 15, each once within a row
- plan: int32 [8], replicated, may hold values from 0 to 7, each once
Outputs:
- input_grads: bfloat16 [2, 8, 768, 5376], P('section', None, 'dp')
- adam_update: float32 [2, 16, 43008], P('section', 'dp')
- first_new: float32 [2, 16, 43008], P('section', 'dp')
- second_new: float32 [2, 16, 43008], P('section', 'dp')
Inputs may be any that keep to these rules, and one draw needn't show every extreme that they name: `old_owner`: the entries of one section's row are distinct.
All inputs are finite; a program needn't handle non-finite values.
Results may differ from a plain program's by a relative error of at most 0.025.
Values may be sent and summed in bfloat16 or wider, within the bound.
A program may use at most 64 MiB of HBM per device.

v0:
```python
import jax
import jax.numpy as jnp
from jax import lax
from jax.sharding import PartitionSpec as P

beta_one = 0.9
beta_two = 0.95
adam_eps = 1e-08
adam_step = 1000.0
loss_scale = 4096.0


def passed_along(value, axis, steps):
    count = lax.axis_size(axis)
    first, last = (max(0, -steps), min(count, count - steps))
    return lax.ppermute(value, axis, [(source, source + steps) for source in range(first, last)])


def silu_slope(pre_value):
    gate_value = jax.nn.sigmoid(pre_value)
    return gate_value * (1.0 + pre_value * (1.0 - gate_value))


def per_device(
    activations,
    loss_grads,
    adapter_in,
    adapter_out,
    first_moment,
    second_moment,
    old_owner,
    new_owner,
    plan,
):
    sections = lax.axis_size("section")
    section_index = lax.axis_index("section")
    replicas = lax.axis_size("dp")
    my_index = lax.axis_index("dp")
    weight_in = adapter_in[0]
    weight_out = adapter_out[0]
    inputs_all = activations[0]
    micro_count = inputs_all.shape[0]
    tok_rows = inputs_all.shape[1]
    width = inputs_all.shape[2]
    owners_old = old_owner[0]
    owners_new = new_owner[0]
    block_len = first_moment.shape[2] // 2
    replica_ids = jnp.arange(replicas, dtype=jnp.int32)
    new_block = jnp.sum(jnp.where(owners_new == my_index, replica_ids, 0))

    def drain_turn(turn_index, state):
        previous, grad_in, grad_out, emitted = state
        received = passed_along(previous, "section", -1)
        slot = turn_index - (sections - 1 - section_index)
        is_valid = (slot >= 0) & (slot < micro_count)
        clamped = jnp.clip(slot, 0, micro_count - 1)
        micro = lax.dynamic_index_in_dim(plan, clamped, 0, keepdims=False)
        section_input = lax.dynamic_index_in_dim(inputs_all, micro, 0, keepdims=False)
        from_loss = lax.dynamic_index_in_dim(loss_grads, micro, 0, keepdims=False)
        incoming = jnp.where(section_index == sections - 1, from_loss, received)
        pre_value = jnp.dot(section_input, weight_in, preferred_element_type=jnp.float32)
        hidden = jax.nn.silu(pre_value).astype(jnp.bfloat16)
        act_grad = jnp.dot(incoming, weight_out.T, preferred_element_type=jnp.float32)
        pre_grad = (act_grad * silu_slope(pre_value)).astype(jnp.bfloat16)
        input_grad = (
            incoming.astype(jnp.float32)
            + jnp.dot(pre_grad, weight_in.T, preferred_element_type=jnp.float32)
        ).astype(jnp.bfloat16)
        valid_weight = is_valid.astype(jnp.float32)
        grad_in = grad_in + valid_weight * jnp.dot(
            section_input.T, pre_grad, preferred_element_type=jnp.float32
        )
        grad_out = grad_out + valid_weight * jnp.dot(
            hidden.T, incoming, preferred_element_type=jnp.float32
        )
        earlier = lax.dynamic_index_in_dim(emitted, clamped, 0, keepdims=False)
        written = jnp.where(is_valid, input_grad, earlier)
        emitted = lax.dynamic_update_index_in_dim(emitted, written, clamped, 0)
        return (input_grad, grad_in, grad_out, emitted)

    start_state = (
        jnp.zeros((tok_rows, width), jnp.bfloat16),
        jnp.zeros(weight_in.shape, jnp.float32),
        jnp.zeros(weight_out.shape, jnp.float32),
        jnp.zeros((micro_count, tok_rows, width), jnp.bfloat16),
    )
    last_grad, grad_in, grad_out, emitted = lax.fori_loop(
        0, micro_count + sections - 1, drain_turn, start_state
    )
    partial_value = jnp.concatenate([grad_in.reshape(-1), grad_out.reshape(-1)])
    totals = lax.psum(partial_value, "dp")
    grads = lax.dynamic_slice_in_dim(totals, new_block * block_len, block_len) / loss_scale
    old_count = owners_old.shape[0]
    piece_len = 2 * block_len // replicas
    first_pieces = first_moment[0, 0].reshape(replicas, piece_len)
    second_pieces = second_moment[0, 0].reshape(replicas, piece_len)
    first_spread = lax.all_to_all(first_pieces, "dp", split_axis=0, concat_axis=0, tiled=True)
    second_spread = lax.all_to_all(second_pieces, "dp", split_axis=0, concat_axis=0, tiled=True)
    first_held = jnp.take(first_spread, owners_old, axis=0)
    second_held = jnp.take(second_spread, owners_old, axis=0)
    my_half = my_index // old_count
    targets = owners_new.reshape(-1, 2)
    target_of_block = jnp.where(my_half == 0, targets[:, 0], targets[:, 1])
    picker = (target_of_block[None, :] == replica_ids[:, None]).astype(jnp.float32)
    first_out = jnp.dot(picker, first_held, precision=lax.Precision.HIGHEST)
    second_out = jnp.dot(picker, second_held, precision=lax.Precision.HIGHEST)
    first_got = lax.all_to_all(first_out, "dp", split_axis=0, concat_axis=0, tiled=True)
    second_got = lax.all_to_all(second_out, "dp", split_axis=0, concat_axis=0, tiled=True)
    half_start = new_block % 2 * old_count
    first_mine = lax.dynamic_slice_in_dim(first_got, half_start, old_count, 0).reshape(-1)
    second_mine = lax.dynamic_slice_in_dim(second_got, half_start, old_count, 0).reshape(-1)
    moved = (first_mine, second_mine)
    first_old, second_old = moved
    first_next = beta_one * first_old + (1.0 - beta_one) * grads
    second_next = beta_two * second_old + (1.0 - beta_two) * grads * grads
    update = (
        first_next
        / (1.0 - beta_one**adam_step)
        / (jnp.sqrt(second_next / (1.0 - beta_two**adam_step)) + adam_eps)
    )
    return (emitted[None], update[None, None], first_next[None, None], second_next[None, None])


def solution(mesh):
    placed = (
        P("section", None, "dp", None),
        P(None, "dp", None),
        P("section", None, None),
        P("section", None, None),
        P("section", "dp", None),
        P("section", "dp", None),
        P("section", None),
        P("section", None),
        P(),
    )
    return jax.shard_map(
        per_device,
        mesh=mesh,
        in_specs=placed,
        out_specs=(
            P("section", None, "dp", None),
            P("section", "dp", None),
            P("section", "dp", None),
            P("section", "dp", None),
        ),
        check_vma=False,
    )
```

profile of v0, /device:TPU:0, one launch (start us, length us, event | category | flops | bytes accessed | tf_op | source)
XLA Modules:
  0.0 360.3 jit_solution(12223333010346438085)
XLA Ops:
  7.2 7.6 %all-to-all-start.2 = ((f32[16,1,5376]{2,1,0:T(1,128)}), f32[16,1,5376]{2,1,0:T(1,128)S(1)}, u32[]{:S(2)}, u32[]{:S(2)}) async-start(f32[16,1,5376]{2,1,0:T(1,128)} %bitcast.84), calls=%async_computation.2 | async-start | bytes 688128 | tf_op jit(solution)/shard_map/all_to_all | solution.py:98
  17.8 8.3 %all-to-all-done.2 = f32[16,1,5376]{2,1,0:T(1,128)S(1)} async-done(((f32[16,1,5376]{2,1,0:T(1,128)}), f32[16,1,5376]{2,1,0:T(1,128)S(1)}, u32[]{:S(2)}, u32[]{:S(2)}) %all-to-all-start.2) | async-done | bytes 344096 | tf_op jit(solution)/shard_map/all_to_all | solution.py:98
  26.1 4.2 %all-to-all-start = ((f32[16,1,5376]{2,1,0:T(1,128)}), f32[16,1,5376]{2,1,0:T(1,128)}, u32[]{:S(2)}, u32[]{:S(2)}) async-start(f32[16,1,5376]{2,1,0:T(1,128)} %bitcast.5), calls=%async_computation | async-start | bytes 688128 | tf_op jit(solution)/shard_map/all_to_all | solution.py:97
  30.3 2.3 broadcast_in_dim.52
  32.6 192.7 %while.22 = (s32[]{:T(128)}, bf16[48,5376]{1,0:T(8,128)(2,1)}, f32[5376,64]{0,1:T(8,128)S(1)}, f32[64,5376]{1,0:T(8,128)}, bf16[8,48,5376]{2,1,0:T(8,128)(2,1)},...) while((s32[]{:T(128)}, bf16[48,5376]{1,0:T(8,128)(2,1)}, ...), condition=%wide.region_1.2_spmd.clone, body=%wide.region_0.1_spmd.clone.sunk | while | flops 168806416 | bytes 28440968 | solution.py:87
  39.9 9.6 %collective-permute-done = bf16[48,5376]{1,0:T(8,128)(2,1)} collective-permute-done((bf16[48,5376]{1,0:T(8,128)(2,1)}, bf16[48,5376]{1,0:T(8,128)(2,1)}, u32[]{:S(2)}, u32[]{:S(2)}) %collective-permute-start) | collective-permute-done | bytes 516128 | tf_op jit(solution)/shard_map/while/body/eval_jaxpr/ppermute | solution.py:16
  52.7 1.7 fusion.54
  56.1 1.9 broadcast_select_fusion.2
  64.5 8.7 %collective-permute-done = bf16[48,5376]{1,0:T(8,128)(2,1)} collective-permute-done((bf16[48,5376]{1,0:T(8,128)(2,1)}, bf16[48,5376]{1,0:T(8,128)(2,1)}, u32[]{:S(2)}, u32[]{:S(2)}) %collective-permute-start) | collective-permute-done | bytes 516128 | tf_op jit(solution)/shard_map/while/body/eval_jaxpr/ppermute | solution.py:16
  79.8 1.9 broadcast_select_fusion.2
  88.1 7.9 %collective-permute-done = bf16[48,5376]{1,0:T(8,128)(2,1)} collective-permute-done((bf16[48,5376]{1,0:T(8,128)(2,1)}, bf16[48,5376]{1,0:T(8,128)(2,1)}, u32[]{:S(2)}, u32[]{:S(2)}) %collective-permute-start) | collective-permute-done | bytes 516128 | tf_op jit(solution)/shard_map/while/body/eval_jaxpr/ppermute | solution.py:16
  102.6 1.9 broadcast_select_fusion.2
  111.0 7.0 %collective-permute-done = bf16[48,5376]{1,0:T(8,128)(2,1)} collective-permute-done((bf16[48,5376]{1,0:T(8,128)(2,1)}, bf16[48,5376]{1,0:T(8,128)(2,1)}, u32[]{:S(2)}, u32[]{:S(2)}) %collective-permute-start) | collective-permute-done | bytes 516128 | tf_op jit(solution)/shard_map/while/body/eval_jaxpr/ppermute | solution.py:16
  124.6 1.9 broadcast_select_fusion.2
  132.9 6.2 %collective-permute-done = bf16[48,5376]{1,0:T(8,128)(2,1)} collective-permute-done((bf16[48,5376]{1,0:T(8,128)(2,1)}, bf16[48,5376]{1,0:T(8,128)(2,1)}, u32[]{:S(2)}, u32[]{:S(2)}) %collective-permute-start) | collective-permute-done | bytes 516128 | tf_op jit(solution)/shard_map/while/body/eval_jaxpr/ppermute | solution.py:16
  145.7 1.9 broadcast_select_fusion.2
  154.1 5.3 %collective-permute-done = bf16[48,5376]{1,0:T(8,128)(2,1)} collective-permute-done((bf16[48,5376]{1,0:T(8,128)(2,1)}, bf16[48,5376]{1,0:T(8,128)(2,1)}, u32[]{:S(2)}, u32[]{:S(2)}) %collective-permute-start) | collective-permute-done | bytes 516128 | tf_op jit(solution)/shard_map/while/body/eval_jaxpr/ppermute | solution.py:16
  166.0 1.9 broadcast_select_fusion.2
  174.4 4.8 %collective-permute-done = bf16[48,5376]{1,0:T(8,128)(2,1)} collective-permute-done((bf16[48,5376]{1,0:T(8,128)(2,1)}, bf16[48,5376]{1,0:T(8,128)(2,1)}, u32[]{:S(2)}, u32[]{:S(2)}) %collective-permute-start) | collective-permute-done | bytes 516128 | tf_op jit(solution)/shard_map/while/body/eval_jaxpr/ppermute | solution.py:16
  182.3 1.7 fusion.54
  185.8 1.9 broadcast_select_fusion.2
  194.1 4.8 %collective-permute-done = bf16[48,5376]{1,0:T(8,128)(2,1)} collective-permute-done((bf16[48,5376]{1,0:T(8,128)(2,1)}, bf16[48,5376]{1,0:T(8,128)(2,1)}, u32[]{:S(2)}, u32[]{:S(2)}) %collective-permute-start) | collective-permute-done | bytes 516128 | tf_op jit(solution)/shard_map/while/body/eval_jaxpr/ppermute | solution.py:16
  205.5 1.9 broadcast_select_fusion.2
  213.9 4.8 %collective-permute-done = bf16[48,5376]{1,0:T(8,128)(2,1)} collective-permute-done((bf16[48,5376]{1,0:T(8,128)(2,1)}, bf16[48,5376]{1,0:T(8,128)(2,1)}, u32[]{:S(2)}, u32[]{:S(2)}) %collective-permute-start) | collective-permute-done | bytes 516128 | tf_op jit(solution)/shard_map/while/body/eval_jaxpr/ppermute | solution.py:16
  226.7 2.1 copy.18
  228.8 2.9 reshape.52
  234.0 5.3 %all-to-all-start.3 = ((f32[16,1,5376]{2,1,0:T(1,128)}), f32[16,1,5376]{2,1,0:T(1,128)S(1)}, u32[]{:S(2)}, u32[]{:S(2)}) async-start(f32[16,1,5376]{2,1,0:T(1,128)} %copy.19), calls=%async_computation.3 | async-start | bytes 688128 | tf_op jit(solution)/shard_map/all_to_all | solution.py:108
  239.3 1.8 pad_maximum_fusion
  247.4 3.2 all-to-all-done.3
  250.6 3.5 all-to-all-start.1
  254.3 15.2 %all-to-all-done.1 = f32[16,1,5376]{2,1,0:T(1,128)S(1)} async-done(((f32[16,1,5376]{2,1,0:T(1,128)}), f32[16,1,5376]{2,1,0:T(1,128)S(1)}, u32[]{:S(2)}, u32[]{:S(2)}) %all-to-all-start.1) | async-done | bytes 344096 | tf_op jit(solution)/shard_map/all_to_all | solution.py:107
  269.7 82.0 %all-reduce.2.cloned.1.call-done = f32[688128]{0:T(1024)} async-done(((f32[688128]{0:T(1024)}), f32[688128]{0:T(1024)}) %all-reduce.2.cloned.1.call-update) | async-done | bytes 2752528 | tf_op jit(solution)/shard_map/psum | solution.py:91
  (157 shorter events, 108.5 us)
Async XLA Ops:
  7.2 9.9 %copy-start.8 = (s32[1,16]{1,0:T(1,128)S(1)}, s32[1,16]{1,0:T(1,128)}, u32[]{:S(2)}) copy-start(s32[1,16]{1,0:T(1,128)} %param.20) | copy-start | bytes 196
  7.2 10.6 %copy-start.7 = (s32[1,8]{1,0:T(1,128)S(1)}, s32[1,8]{1,0:T(1,128)}, u32[]{:S(2)}) copy-start(s32[1,8]{1,0:T(1,128)} %param.19) | copy-start | bytes 100
  7.2 18.9 %all-to-all-start.2 = ((f32[16,1,5376]{2,1,0:T(1,128)}), f32[16,1,5376]{2,1,0:T(1,128)S(1)}, u32[]{:S(2)}, u32[]{:S(2)}) async-start(f32[16,1,5376]{2,1,0:T(1,128)} %bitcast.84), calls=%async_computation.2 | async-start | bytes 688128 | tf_op jit(solution)/shard_map/all_to_all | solution.py:98
  26.1 4.2 %copy-start.4 = (f32[16,1,5376]{2,1,0:T(1,128)}, f32[16,1,5376]{2,1,0:T(1,128)S(1)}, u32[]{:S(2)}) copy-start(f32[16,1,5376]{2,1,0:T(1,128)S(1)} %all-to-all-done.2) | copy-start | bytes 1032196
  26.1 207.9 %all-to-all-start = ((f32[16,1,5376]{2,1,0:T(1,128)}), f32[16,1,5376]{2,1,0:T(1,128)}, u32[]{:S(2)}, u32[]{:S(2)}) async-start(f32[16,1,5376]{2,1,0:T(1,128)} %bitcast.5), calls=%async_computation | async-start | bytes 688128 | tf_op jit(solution)/shard_map/all_to_all | solution.py:97
  30.3 2.3 copy-start.2
  30.3 2.3 copy-start.6
  33.4 16.1 %collective-permute-start = (bf16[48,5376]{1,0:T(8,128)(2,1)}, bf16[48,5376]{1,0:T(8,128)(2,1)}, u32[]{:S(2)}, u32[]{:S(2)}) collective-permute-start(bf16[48,5376]{1,0:T(8,128)(2,1)} %broadcast_select_fusion.2), channel_id=1, source_target_pairs={{16,0},{17,1},{18,2},{19,3},{20,4},{21,5},{22,6},{23,7},{24,8},{25... | collective-permute-start | bytes 1548296 | tf_op jit(solution)/shard_map/while/body/eval_jaxpr/ppermute | solution.py:16
  52.7 1.8 copy-start
  55.0 1.1 copy-start.1
  58.0 15.2 %collective-permute-start = (bf16[48,5376]{1,0:T(8,128)(2,1)}, bf16[48,5376]{1,0:T(8,128)(2,1)}, u32[]{:S(2)}, u32[]{:S(2)}) collective-permute-start(bf16[48,5376]{1,0:T(8,128)(2,1)} %broadcast_select_fusion.2), channel_id=1, source_target_pairs={{16,0},{17,1},{18,2},{19,3},{20,4},{21,5},{22,6},{23,7},{24,8},{25... | collective-permute-start | bytes 1548296 | tf_op jit(solution)/shard_map/while/body/eval_jaxpr/ppermute | solution.py:16
  76.4 1.8 copy-start
  78.7 1.1 copy-start.1
  81.7 14.4 %collective-permute-start = (bf16[48,5376]{1,0:T(8,128)(2,1)}, bf16[48,5376]{1,0:T(8,128)(2,1)}, u32[]{:S(2)}, u32[]{:S(2)}) collective-permute-start(bf16[48,5376]{1,0:T(8,128)(2,1)} %broadcast_select_fusion.2), channel_id=1, source_target_pairs={{16,0},{17,1},{18,2},{19,3},{20,4},{21,5},{22,6},{23,7},{24,8},{25... | collective-permute-start | bytes 1548296 | tf_op jit(solution)/shard_map/while/body/eval_jaxpr/ppermute | solution.py:16
  99.2 1.7 copy-start
  104.5 13.5 %collective-permute-start = (bf16[48,5376]{1,0:T(8,128)(2,1)}, bf16[48,5376]{1,0:T(8,128)(2,1)}, u32[]{:S(2)}, u32[]{:S(2)}) collective-permute-start(bf16[48,5376]{1,0:T(8,128)(2,1)} %broadcast_select_fusion.2), channel_id=1, source_target_pairs={{16,0},{17,1},{18,2},{19,3},{20,4},{21,5},{22,6},{23,7},{24,8},{25... | collective-permute-start | bytes 1548296 | tf_op jit(solution)/shard_map/while/body/eval_jaxpr/ppermute | solution.py:16
  121.2 1.7 copy-start
  126.4 12.7 %collective-permute-start = (bf16[48,5376]{1,0:T(8,128)(2,1)}, bf16[48,5376]{1,0:T(8,128)(2,1)}, u32[]{:S(2)}, u32[]{:S(2)}) collective-permute-start(bf16[48,5376]{1,0:T(8,128)(2,1)} %broadcast_select_fusion.2), channel_id=1, source_target_pairs={{16,0},{17,1},{18,2},{19,3},{20,4},{21,5},{22,6},{23,7},{24,8},{25... | collective-permute-start | bytes 1548296 | tf_op jit(solution)/shard_map/while/body/eval_jaxpr/ppermute | solution.py:16
  142.3 1.8 copy-start
  147.6 11.8 %collective-permute-start = (bf16[48,5376]{1,0:T(8,128)(2,1)}, bf16[48,5376]{1,0:T(8,128)(2,1)}, u32[]{:S(2)}, u32[]{:S(2)}) collective-permute-start(bf16[48,5376]{1,0:T(8,128)(2,1)} %broadcast_select_fusion.2), channel_id=1, source_target_pairs={{16,0},{17,1},{18,2},{19,3},{20,4},{21,5},{22,6},{23,7},{24,8},{25... | collective-permute-start | bytes 1548296 | tf_op jit(solution)/shard_map/while/body/eval_jaxpr/ppermute | solution.py:16
  162.6 1.8 copy-start
  167.9 11.3 %collective-permute-start = (bf16[48,5376]{1,0:T(8,128)(2,1)}, bf16[48,5376]{1,0:T(8,128)(2,1)}, u32[]{:S(2)}, u32[]{:S(2)}) collective-permute-start(bf16[48,5376]{1,0:T(8,128)(2,1)} %broadcast_select_fusion.2), channel_id=1, source_target_pairs={{16,0},{17,1},{18,2},{19,3},{20,4},{21,5},{22,6},{23,7},{24,8},{25... | collective-permute-start | bytes 1548296 | tf_op jit(solution)/shard_map/while/body/eval_jaxpr/ppermute | solution.py:16
  182.3 1.8 copy-start
  187.6 11.3 %collective-permute-start = (bf16[48,5376]{1,0:T(8,128)(2,1)}, bf16[48,5376]{1,0:T(8,128)(2,1)}, u32[]{:S(2)}, u32[]{:S(2)}) collective-permute-start(bf16[48,5376]{1,0:T(8,128)(2,1)} %broadcast_select_fusion.2), channel_id=1, source_target_pairs={{16,0},{17,1},{18,2},{19,3},{20,4},{21,5},{22,6},{23,7},{24,8},{25... | collective-permute-start | bytes 1548296 | tf_op jit(solution)/shard_map/while/body/eval_jaxpr/ppermute | solution.py:16
  202.1 1.8 copy-start
  207.4 11.3 %collective-permute-start = (bf16[48,5376]{1,0:T(8,128)(2,1)}, bf16[48,5376]{1,0:T(8,128)(2,1)}, u32[]{:S(2)}, u32[]{:S(2)}) collective-permute-start(bf16[48,5376]{1,0:T(8,128)(2,1)} %broadcast_select_fusion.2), channel_id=1, source_target_pairs={{16,0},{17,1},{18,2},{19,3},{20,4},{21,5},{22,6},{23,7},{24,8},{25... | collective-permute-start | bytes 1548296 | tf_op jit(solution)/shard_map/while/body/eval_jaxpr/ppermute | solution.py:16
  221.8 1.8 copy-start
  228.8 3.1 copy-start.5
  232.5 6.8 %copy-start.3 = (f32[344064]{0:T(1024)S(1)}, f32[344064]{0:T(1024)}, u32[]{:S(2)}) copy-start(f32[344064]{0:T(1024)} %reshape.52) | copy-start | bytes 4128772
  234.0 16.6 %all-to-all-start.3 = ((f32[16,1,5376]{2,1,0:T(1,128)}), f32[16,1,5376]{2,1,0:T(1,128)S(1)}, u32[]{:S(2)}, u32[]{:S(2)}) async-start(f32[16,1,5376]{2,1,0:T(1,128)} %copy.19), calls=%async_computation.3 | async-start | bytes 688128 | tf_op jit(solution)/shard_map/all_to_all | solution.py:108
  239.3 112.5 %all-reduce.2.cloned.1.call-start = ((), (), s32[]{:S(2)}) async-start(), calls=%async_computation.4 | async-start | bytes 5505024 | tf_op jit(solution)/shard_map/psum | solution.py:91
  250.6 18.9 %all-to-all-start.1 = ((f32[16,1,5376]{2,1,0:T(1,128)}), f32[16,1,5376]{2,1,0:T(1,128)S(1)}, u32[]{:S(2)}, u32[]{:S(2)}) async-start(f32[16,1,5376]{2,1,0:T(1,128)} %copy.17), calls=%async_computation.1 | async-start | bytes 688128 | tf_op jit(solution)/shard_map/all_to_all | solution.py:107
  (7 other events, 7.7 us)
Sparse Core Ops, SparseCore 0:
  243.7 108.0 all-reduce.1
where the time goes:
time: 363 us; the launch traced here: 360 us
  waiting for transfers between devices  168 us (46%)
  matrix products  51.1 us (14%)
  local copies, waits for them, and re-layouts  40.9 us (11%)
  other arithmetic  32.4 us (9%)
  starting transfers between devices  32.1 us (9%)
  loops' own time  19.1 us (5%)
  between operations  16.9 us (5%)
    psum x1, waiting for transfers between devices, per_device(): totals = lax.psum(partial_value, 'dp')  82 us
    ppermute x9, waiting for transfers between devices, passed_along(): lax.ppermute(value, axis, [(source, source + steps) for source in range(f...  59.2 us
    another operation x1, loops' own time, per_device(): lax.fori_loop(0, micro_count + sections - 1, drain_turn, start_state)  19.1 us
    while x9, other arithmetic  15.8 us
    dot_general x9, matrix products, drain_turn(): jnp.dot(section_input.T, pre_grad, preferred_element_type=jnp.float32)  15.7 us
    all_to_all x1, waiting for transfers between devices, per_device(): lax.all_to_all(first_out, 'dp', split_axis=0, concat_axis=0, tiled=True)  15.2 us
    dot_general x9, matrix products, drain_turn(): jnp.dot(pre_grad, weight_in.T, preferred_element_type=jnp.float32)  14.3 us
    dot_general x9, matrix products, drain_turn(): jnp.dot(section_input, weight_in, preferred_element_type=jnp.float32)  12.6 us
  transfers between devices with their start and end apart: 14, of which 13 were waited for; matrix products, arithmetic and copies ran while one was open for 31% of the time, Pallas kernels for 0%

commit v1 on v0

--- a/solution.py
+++ b/solution.py
@@ -1,6 +1,11 @@
+import functools
+import math
+
 import jax
 import jax.numpy as jnp
 from jax import lax
+from jax.experimental import pallas as pl
+from jax.experimental.pallas import tpu as pltpu
 from jax.sharding import PartitionSpec as P
 
 beta_one = 0.9
@@ -8,6 +13,350 @@
 adam_eps = 1e-08
 adam_step = 1000.0
 loss_scale = 4096.0
+MESH = pl.DeviceIdType.MESH
+VMEM = pl.BlockSpec(memory_space=pltpu.VMEM)
+SMEM = pl.BlockSpec(memory_space=pltpu.SMEM)
+ANY = pl.BlockSpec(memory_space=pl.ANY)
+
+
+def nt_dot(left, right):
+    return lax.dot_general(left, right, (((1,), (1,)), ((), ())), preferred_element_type=jnp.float32)
+
+
+def column_width(width):
+    return 128 * max(d for d in range(1, 8) if (width // 128) % d == 0)
+
+
+def greet(n, me, extra):
+    barrier = pltpu.get_barrier_semaphore()
+
+    @pl.loop(1, n)
+    def _(d):
+        pl.semaphore_signal(barrier, inc=1, device_id={"dp": lax.rem(me + d, n)}, device_id_type=MESH)
+
+    if extra is not None:
+        pl.semaphore_signal(barrier, inc=1, device_id={"section": extra}, device_id_type=MESH)
+    pl.semaphore_wait(barrier, n - 1 + (extra is not None))
+
+
+def exchange_kernel(
+    n, x_hbm, l_hbm, win_ref, wout_ref, pieces_ref, pick_ref,
+    pre_ref, p_ref, w_ref, got_ref,
+    x_buf, l_buf, p_buf, spread, chosen,
+    x_sem, l_sem, w_send, w_recv, f_send, f_recv, p_send, p_recv, a_send, a_recv, b_send, b_recv, own_sem,
+):
+    me = lax.axis_index("dp")
+    other = 1 - lax.axis_index("section")
+    core = lax.rem(me, 2)
+    sibling = me + 1 - 2 * core
+    rank, width = win_ref.shape
+    cw = column_width(width)
+    chunks = width // cw
+    loads = []
+    for c in range(chunks):
+        cols = pl.ds(c * cw, cw)
+        for src, dst, sem in ((x_hbm, x_buf, x_sem), (l_hbm, l_buf, l_sem)):
+            load = pltpu.make_async_copy(src.at[:, cols], dst.at[:, cols], sem.at[c])
+            load.start()
+            loads.append(load)
+    own = pltpu.make_async_copy(pieces_ref.at[me], spread.at[me], own_sem.at[0])
+    own.start()
+    greet(n, me, other)
+    half = rank // 2
+    mine = pl.ds(pl.multiple_of(core * half, half), half)
+    theirs = pl.ds(pl.multiple_of((1 - core) * half, half), half)
+    w_copy = pltpu.make_async_remote_copy(
+        win_ref.at[mine], w_ref.at[mine], w_send, w_recv, device_id={"section": other}, device_id_type=MESH
+    )
+    w_copy.start()
+
+    def spread_copy(d):
+        peer = lax.rem(me + d, n)
+        return pltpu.make_async_remote_copy(
+            pieces_ref.at[peer], spread.at[me], a_send.at[d], a_recv.at[d],
+            device_id={"dp": peer}, device_id_type=MESH,
+        )
+
+    def spread_arrival(d):
+        peer = lax.rem(me + n - d, n)
+        return pltpu.make_async_remote_copy(
+            pieces_ref.at[peer], spread.at[peer], a_send.at[d], a_recv.at[d],
+            device_id={"dp": peer}, device_id_type=MESH,
+        )
+
+    def gather_copy(d):
+        peer = lax.rem(me + d, n)
+        return pltpu.make_async_remote_copy(
+            chosen.at[peer], got_ref.at[me], b_send.at[d], b_recv.at[d],
+            device_id={"dp": peer}, device_id_type=MESH,
+        )
+
+    def gather_arrival(d):
+        peer = lax.rem(me + n - d, n)
+        return pltpu.make_async_remote_copy(
+            chosen.at[peer], got_ref.at[peer], b_send.at[d], b_recv.at[d],
+            device_id={"dp": peer}, device_id_type=MESH,
+        )
+
+    @pl.loop(1, n)
+    def _(d):
+        spread_copy(d).start()
+
+    rows = x_buf.shape[0]
+    pre = jnp.zeros((rows, rank), jnp.float32)
+    act = jnp.zeros((rows, rank), jnp.float32)
+    for c in range(chunks):
+        cols = pl.ds(c * cw, cw)
+        loads[2 * c].wait()
+        loads[2 * c + 1].wait()
+        pre = pre + nt_dot(x_buf[:, cols], win_ref[:, cols])
+        act = act + nt_dot(l_buf[:, cols], wout_ref[:, cols])
+    pre_ref[...] = pre
+    p_buf[...] = (act * silu_slope(pre)).astype(jnp.bfloat16)
+    p_copy = pltpu.make_async_remote_copy(
+        p_buf, p_ref, p_send, p_recv, device_id={"section": other}, device_id_type=MESH
+    )
+    p_copy.start()
+    own.wait()
+
+    @pl.loop(1, n)
+    def _(d):
+        spread_arrival(d).wait_recv()
+
+    for t in range(n):
+        chosen[t] = spread[pick_ref[t, 0], pick_ref[t, 1]]
+
+    @pl.loop(1, n)
+    def _(d):
+        gather_copy(d).start()
+
+    keep = pltpu.make_async_copy(chosen.at[me], got_ref.at[me], own_sem.at[1])
+    keep.start()
+    w_copy.wait_recv()
+    forward = pltpu.make_async_remote_copy(
+        w_ref.at[mine], w_ref.at[mine], f_send, f_recv, device_id={"dp": sibling}, device_id_type=MESH
+    )
+    forward.start()
+    w_copy.wait_send()
+    p_copy.wait()
+    forward.wait_send()
+    pltpu.make_async_remote_copy(
+        w_ref.at[theirs], w_ref.at[theirs], f_send, f_recv, device_id={"dp": sibling}, device_id_type=MESH
+    ).wait_recv()
+    keep.wait()
+
+    @pl.loop(1, n)
+    def _(d):
+        spread_copy(d).wait_send()
+        gather_copy(d).wait_send()
+        gather_arrival(d).wait_recv()
+
+
+def exchange(n, x, loss, win, wout, pieces, picks):
+    rows, width = x.shape
+    rank = win.shape[0]
+    chunks = width // column_width(width)
+    dma = pltpu.SemaphoreType.DMA
+    return pl.pallas_call(
+        functools.partial(exchange_kernel, n),
+        out_shape=(
+            jax.ShapeDtypeStruct((rows, rank), jnp.float32),
+            jax.ShapeDtypeStruct((rows, rank), jnp.bfloat16),
+            jax.ShapeDtypeStruct((rank, width), jnp.bfloat16),
+            jax.ShapeDtypeStruct((n,) + pieces.shape[2:], jnp.bfloat16),
+        ),
+        in_specs=[ANY, ANY, VMEM, VMEM, VMEM, SMEM],
+        out_specs=(VMEM,) * 4,
+        scratch_shapes=[
+            pltpu.VMEM(x.shape, jnp.bfloat16),
+            pltpu.VMEM(x.shape, jnp.bfloat16),
+            pltpu.VMEM((rows, rank), jnp.bfloat16),
+            pltpu.VMEM(pieces.shape, jnp.bfloat16),
+            pltpu.VMEM((n,) + pieces.shape[2:], jnp.bfloat16),
+            dma((chunks,)), dma((chunks,)), dma, dma, dma, dma, dma, dma,
+            dma((n,)), dma((n,)), dma((n,)), dma((n,)), dma((2,)),
+        ],
+        compiler_params=pltpu.CompilerParams(collective_id=0, has_side_effects=True),
+        name="exchange",
+    )(x, loss, win, wout, pieces, picks)
+
+
+def drain_kernel(
+    n, relayed_ref, slot_ref, place_ref, x_hbm, l_hbm, pre_ref, p_in_ref, w_up_ref, win_ref, wout_ref,
+    out_hbm, q_ref,
+    x_buf, l_buf, o_buf, gin, gout, turn, x_sem, l_sem, o_sem,
+):
+    rank, width = win_ref.shape
+    micro_count, tok_rows, _ = out_hbm.shape
+    cw = column_width(width)
+    chunks = width // cw
+    loads_x, loads_l = [], []
+    for c in range(chunks):
+        cols = pl.ds(c * cw, cw)
+        loads_l.append(pltpu.make_async_copy(l_hbm.at[:, cols], l_buf.at[:, cols], l_sem.at[c]))
+        loads_l[-1].start()
+    for c in range(chunks):
+        cols = pl.ds(c * cw, cw)
+        loads_x.append(pltpu.make_async_copy(x_hbm.at[:, cols], x_buf.at[:, cols], x_sem.at[c]))
+        loads_x[-1].start()
+    is_relayed = relayed_ref[0] != 0
+    act = jnp.zeros((x_buf.shape[0], rank), jnp.float32)
+    p_in = jnp.where(is_relayed, p_in_ref[...].astype(jnp.float32), 0.0).astype(jnp.bfloat16)
+    for c in range(chunks):
+        cols = pl.ds(c * cw, cw)
+        loads_l[c].wait()
+        relayed = l_buf[:, cols].astype(jnp.float32) + jnp.dot(
+            p_in, w_up_ref[:, cols], preferred_element_type=jnp.float32
+        )
+        incoming = relayed.astype(jnp.bfloat16)
+        l_buf[:, cols] = incoming
+        act = act + nt_dot(incoming, wout_ref[:, cols])
+    pre = pre_ref[...]
+    hidden_t = jax.nn.silu(pre).T.astype(jnp.bfloat16)
+    grad = act * silu_slope(pre)
+    p_now = grad.astype(jnp.bfloat16)
+    p_t = grad.T.astype(jnp.bfloat16)
+    stores = []
+    for c in range(chunks):
+        cols = pl.ds(c * cw, cw)
+        loads_x[c].wait()
+        incoming = l_buf[:, cols]
+        o_buf[:, cols] = (
+            incoming.astype(jnp.float32) + jnp.dot(p_now, win_ref[:, cols], preferred_element_type=jnp.float32)
+        ).astype(jnp.bfloat16)
+        for m in range(micro_count):
+            store = pltpu.make_async_copy(
+                o_buf.at[pl.ds(m * tok_rows, tok_rows), cols],
+                out_hbm.at[slot_ref[m], :, cols],
+                o_sem.at[c, m],
+            )
+            store.start()
+            stores.append(store)
+        gin[cols, :] = jnp.dot(p_t, x_buf[:, cols], preferred_element_type=jnp.float32).T
+        gout[:, cols] = jnp.dot(hidden_t, incoming, preferred_element_type=jnp.float32)
+    block_rows = q_ref.shape[1]
+    tiles = width // 128
+    for b in range(n // 2):
+        start = b * block_rows * 2
+        low = gin[pl.ds(start, block_rows, stride=2), :]
+        high = gin[pl.ds(start + 1, block_rows, stride=2), :]
+        q_ref[place_ref[b]] = jnp.concatenate([low, high], axis=1).astype(jnp.bfloat16)
+    lines = block_rows // tiles
+    for b in range(n // 2):
+        for t in range(tiles):
+            turn[pl.ds(t, lines, stride=tiles), :] = gout[b * lines : (b + 1) * lines, t * 128 : (t + 1) * 128]
+        q_ref[place_ref[n // 2 + b]] = turn[...].astype(jnp.bfloat16)
+    for store in stores:
+        store.wait()
+
+
+def drain(n, block_len, micro_count, relayed, slots, places, x, loss, pre, p_in, w_up, win, wout):
+    rows, width = x.shape
+    rank = win.shape[0]
+    chunks = width // column_width(width)
+    dma = pltpu.SemaphoreType.DMA
+    return pl.pallas_call(
+        functools.partial(drain_kernel, n),
+        out_shape=(
+            jax.ShapeDtypeStruct((micro_count, rows // micro_count, width), jnp.bfloat16),
+            jax.ShapeDtypeStruct((n, block_len // 128, 128), jnp.bfloat16),
+        ),
+        in_specs=[SMEM, SMEM, SMEM, ANY, ANY, VMEM, VMEM, VMEM, VMEM, VMEM],
+        out_specs=(ANY, VMEM),
+        scratch_shapes=[
+            pltpu.VMEM(x.shape, jnp.bfloat16),
+            pltpu.VMEM(x.shape, jnp.bfloat16),
+            pltpu.VMEM(x.shape, jnp.bfloat16),
+            pltpu.VMEM((width, rank), jnp.float32),
+            pltpu.VMEM((rank, width), jnp.float32),
+            pltpu.VMEM((block_len // 128, 128), jnp.float32),
+            dma((chunks,)), dma((chunks,)), dma((chunks, micro_count)),
+        ],
+        name="drain",
+    )(relayed, slots, places, x, loss, pre, p_in, w_up, win, wout)
+
+
+def reduce_kernel(
+    n, q_ref, m_ref, v_ref, u_ref, first_ref, second_ref,
+    near, summed, far, s1, r1, s2, r2,
+):
+    me = lax.axis_index("dp")
+    core = lax.rem(me, 2)
+    chip = me // 2
+    chips = n // 2
+    sibling = me + 1 - 2 * core
+    greet(n, me, None)
+
+    def near_copy(d):
+        to = lax.rem(chip + d, chips)
+        return pltpu.make_async_remote_copy(
+            q_ref.at[(1 - core) * chips + to], near.at[to], s1.at[d], r1.at[d],
+            device_id={"dp": sibling}, device_id_type=MESH,
+        )
+
+    def far_copy(d):
+        to = lax.rem(chip + d, chips)
+        return pltpu.make_async_remote_copy(
+            summed.at[to], far.at[d], s2.at[d], r2.at[d],
+            device_id={"dp": to * 2 + core}, device_id_type=MESH,
+        )
+
+    @pl.loop(1, chips + 1)
+    def _(step):
+        near_copy(lax.rem(step, chips)).start()
+
+    @pl.loop(1, chips)
+    def _(d):
+        to = lax.rem(chip + d, chips)
+        near_copy(d).wait_recv()
+        summed[to] = (
+            q_ref[core * chips + to].astype(jnp.float32) + near[to].astype(jnp.float32)
+        ).astype(jnp.bfloat16)
+        far_copy(d).start()
+
+    near_copy(0).wait_recv()
+    total = q_ref[core * chips + chip].astype(jnp.float32) + near[chip].astype(jnp.float32)
+    first_ref[...] = total
+
+    @pl.loop(1, chips)
+    def _(d):
+        far_copy(d).wait_recv()
+        first_ref[...] += far[d].astype(jnp.float32)
+
+    grads = first_ref[...] / loss_scale
+    first_next = beta_one * m_ref[...] + (1.0 - beta_one) * grads
+    second_next = beta_two * v_ref[...] + (1.0 - beta_two) * grads * grads
+    first_ref[...] = first_next
+    second_ref[...] = second_next
+    u_ref[...] = (
+        first_next
+        / (1.0 - beta_one**adam_step)
+        / (jnp.sqrt(second_next / (1.0 - beta_two**adam_step)) + adam_eps)
+    )
+
+    @pl.loop(0, chips)
+    def _(d):
+        near_copy(d).wait_send()
+
+    @pl.loop(1, chips)
+    def _(d):
+        far_copy(d).wait_send()
+
+
+def reduce_adam(n, blocks, m, v):
+    lines = m.shape
+    dma = pltpu.SemaphoreType.DMA
+    shape = jax.ShapeDtypeStruct(lines, jnp.float32)
+    group = pltpu.VMEM((n // 2,) + lines, jnp.bfloat16)
+    return pl.pallas_call(
+        functools.partial(reduce_kernel, n),
+        out_shape=(shape,) * 3,
+        in_specs=[VMEM] * 3,
+        out_specs=(VMEM,) * 3,
+        scratch_shapes=[group, group, group] + [dma((n // 2,))] * 4,
+        compiler_params=pltpu.CompilerParams(collective_id=1, has_side_effects=True),
+        name="reduce_adam",
+    )(blocks, m, v)
 
 
 def passed_along(value, axis, steps):
@@ -84,12 +433,46 @@
         jnp.zeros(weight_out.shape, jnp.float32),
         jnp.zeros((micro_count, tok_rows, width), jnp.bfloat16),
     )
+    place_of_block = owners_new % 2 * (replicas // 2) + owners_new // 2
+    lines = (block_len // 128, 128)
+    if sections == 2:
+        rows = micro_count * tok_rows
+        flat_inputs = inputs_all.reshape(rows, width)
+        flat_loss = loss_grads.reshape(rows, width)
+        turned_in = weight_in.T
+        piece_len = block_len // replicas
+        lanes = math.gcd(2 * piece_len, 128)
+        pieces = jnp.stack([first_moment[0, 0], second_moment[0, 0]]).astype(jnp.bfloat16)
+        pieces = pieces.reshape(2, 2, replicas, piece_len).transpose(2, 1, 0, 3)
+        pieces = pieces.reshape(replicas, 2, 2 * piece_len // lanes, lanes)
+        block_of = jnp.sum(
+            jnp.where(owners_new[None, :] == replica_ids[:, None], replica_ids[None, :], 0), axis=1
+        )
+        holder = owners_old[block_of // 2]
+        picks = jnp.stack([holder, block_of % 2], axis=1)
+        pre, p_up, w_up, got = exchange(
+            replicas, flat_inputs, flat_loss, turned_in, weight_out, pieces, picks
+        )
+        slot_ids = jnp.arange(micro_count, dtype=jnp.int32)
+        slots = jnp.sum(jnp.where(plan[None, :] == slot_ids[:, None], slot_ids[None, :], 0), axis=1)
+        relayed = (section_index < sections - 1).astype(jnp.int32).reshape(1)
+        emitted, blocks = drain(
+            replicas, block_len, micro_count, relayed, slots, place_of_block,
+            flat_inputs, flat_loss, pre, p_up, w_up, turned_in, weight_out,
+        )
+        got = got.reshape(replicas, 2, piece_len).astype(jnp.float32)
+        first_old, second_old = (got[:, 0].reshape(lines), got[:, 1].reshape(lines))
+        update, first_next, second_next = reduce_adam(replicas, blocks, first_old, second_old)
+        shape = (1, 1, block_len)
+        return (emitted[None], update.reshape(shape), first_next.reshape(shape), second_next.reshape(shape))
     last_grad, grad_in, grad_out, emitted = lax.fori_loop(
         0, micro_count + sections - 1, drain_turn, start_state
     )
     partial_value = jnp.concatenate([grad_in.reshape(-1), grad_out.reshape(-1)])
-    totals = lax.psum(partial_value, "dp")
-    grads = lax.dynamic_slice_in_dim(totals, new_block * block_len, block_len) / loss_scale
+    block_at = jnp.sum(
+        jnp.where(place_of_block[None, :] == replica_ids[:, None], replica_ids[None, :], 0), axis=1
+    )
+    blocks = jnp.take(partial_value.astype(jnp.bfloat16).reshape((replicas,) + lines), block_at, axis=0)
     old_count = owners_old.shape[0]
     piece_len = 2 * block_len // replicas
     first_pieces = first_moment[0, 0].reshape(replicas, piece_len)
@@ -109,16 +492,11 @@
     half_start = new_block % 2 * old_count
     first_mine = lax.dynamic_slice_in_dim(first_got, half_start, old_count, 0).reshape(-1)
     second_mine = lax.dynamic_slice_in_dim(second_got, half_start, old_count, 0).reshape(-1)
-    moved = (first_mine, second_mine)
-    first_old, second_old = moved
-    first_next = beta_one * first_old + (1.0 - beta_one) * grads
-    second_next = beta_two * second_old + (1.0 - beta_two) * grads * grads
-    update = (
-        first_next
-        / (1.0 - beta_one**adam_step)
-        / (jnp.sqrt(second_next / (1.0 - beta_two**adam_step)) + adam_eps)
-    )
-    return (emitted[None], update[None, None], first_next[None, None], second_next[None, None])
+    update, first_next, second_next = reduce_adam(
+        replicas, blocks, first_mine.reshape(lines), second_mine.reshape(lines)
+    )
+    shape = (1, 1, block_len)
+    return (emitted[None], update.reshape(shape), first_next.reshape(shape), second_next.reshape(shape))
 
 
 def solution(mesh):

time: 363 us -> 75.5 us (0.21)
  the two profiles are of different devices: /device:TPU:0 before, /device:TPU:15 now
where the time goes in v1:
time: 75.5 us; the launch traced here: 75.1 us
  Pallas kernels  58.6 us (78%)
  local copies, waits for them, and re-layouts  9.28 us (12%)
  other arithmetic  6.48 us (9%)
  between operations  0.76 us (1%)
    pallas_call x1, Pallas kernels, reduce_adam(): pl.pallas_call(functools.partial(reduce_kernel, n), out_shape=(shape,) *...  23.5 us
    pallas_call x1, Pallas kernels, exchange(): pl.pallas_call(functools.partial(exchange_kernel, n), out_shape=(jax.Shap...  23 us
    pallas_call x1, Pallas kernels, drain(): pl.pallas_call(functools.partial(drain_kernel, n), out_shape=(jax.ShapeDt...  12.1 us
    unnamed x11, local copies, waits for them, and re-layouts  4.81 us
    another operation x2, other arithmetic  3.74 us

profile of v1, /device:TPU:15, one launch (start us, length us, event | category | flops | bytes accessed | tf_op | source)
XLA Modules:
  0.0 75.1 jit_solution(9735677922893169186)
XLA Ops:
  0.6 0.0 copy-start
  0.6 0.8 %select_reduce_fusion = s32[16]{0:T(128)S(1)} fusion(s32[16]{0:T(128)} %bitcast.54), kind=kLoop, calls=%fused_computation.4 | loop fusion | flops 752 | bytes 128 | tf_op jit(solution)/shard_map/reduce_sum | solution.py:448
  1.5 0.0 copy-done
  1.5 0.7 gather_fusion
  2.1 0.7 copy.34.pick_ref
  2.8 1.9 %convert_reduce_fusion.1 = bf16[86016]{0:T(1024)(128)(2,1)S(1)} fusion(f32[1,1,86016]{2,1,0:T(1,128)} %param.13), kind=kLoop, calls=%fused_computation.3 | loop fusion | flops 86016 | bytes 516096 | tf_op jit(solution)/shard_map/convert.5
  4.7 0.2 stack.14
  4.9 0.3 copy.32
  5.2 1.9 %convert_reduce_fusion = bf16[86016]{0:T(1024)(128)(2,1)S(1)} fusion(f32[1,1,86016]{2,1,0:T(1,128)} %param.14), kind=kLoop, calls=%fused_computation.2 | loop fusion | flops 86016 | bytes 516096 | tf_op jit(solution)/shard_map/convert.4
  7.1 0.2 stack.15
  7.3 0.3 copy.33
  7.6 0.8 %maximum_bitcast_fusion = bf16[16,2,2,2688]{3,2,1,0:T(2,128)(2,1)S(1)} fusion(bf16[1,2,16,2688]{3,0,1,2:T(2,128)(2,1)S(1)} %copy.33, bf16[1,2,16,2688]{3,0,1,2:T(2,128)(2,1)S(1)} %copy.32), kind=kLoop, calls=%fused_computation.1 | loop fusion | flops 688128 | bytes 688128 | tf_op jit(solution)/shard_map/transpose | solution.py:446
  8.4 1.0 %reshape.123.pieces_ref = bf16[16,2,42,128]{3,2,1,0:T(8,128)(2,1)} reshape(bf16[16,2,2,2688]{3,2,1,0:T(2,128)(2,1)S(1)} %maximum_bitcast_fusion) | data formatting | bytes 688128 | tf_op jit(solution)/shard_map/reshape | solution.py:447
  9.3 0.0 copy-start.2
  9.3 0.0 copy-start.3
  9.3 23.0 %exchange.1 = (f32[384,64]{1,0:T(8,128)}, bf16[384,64]{1,0:T(8,128)(2,1)}, bf16[64,5376]{1,0:T(8,128)(2,1)}, bf16[16,42,128]{2,1,0:T(8,128)(2,1)}) custom-call(bf16[384,5376]{1,0:T(8,128)(2,1)} %bitcast.39, bf16[384,5376]{1,0:T(8,128)(2,1)} %bitcast.41, bf16[64,5376]{1,0:T(8,128)(2,1)} %bitcast.43, bf16[64,5376]{1,0:T(8,128)(2,1)} %bitcast.45, ...), custom_call_target="tpu_custom_call" | custom-call | tf_op jit(solution)/shard_map/exchange/pallas_call | solution.py:160
  32.3 0.0 copy-done.2
  32.3 0.5 fusion.1.place_ref
  32.9 0.0 copy-done.3
  32.9 0.6 select_reduce_fusion.1.slot_ref
  33.5 0.0 copy-start.1
  33.5 12.1 %drain.1 = (bf16[8,48,5376]{2,1,0:T(8,128)(2,1)}, bf16[16,336,128]{2,1,0:T(8,128)(2,1)}) custom-call(s32[1]{0:T(128)} %bitcast.relayed_ref, s32[8]{0:T(128)} %select_reduce_fusion.1.slot_ref, s32[16]{0:T(128)} %fusion.1.place_ref, bf16[384,5376]{1,0:T(8,128)(2,1)} %bitcast.40, bf16[384,5376]{1,0:T(8,128)(2,1)} %bitcast.42, ...), custom_call_target="tpu_custom_call" | custom-call | tf_op jit(solution)/shard_map/drain/pallas_call | solution.py:258
  45.6 0.0 copy-done.1
  45.6 0.2 reshape.129
  45.8 1.0 %fusion.3 = (f32[16,1,2688]{2,1,0:T(1,128)}, f32[16,1,2688]{2,1,0:T(1,128)}) fusion(f32[16,2,2688]{2,1,0:T(2,128)S(1)} %reshape.129), kind=kLoop, calls=%fused_computation.25 | loop fusion | bytes 688128 | tf_op jit(solution)/shard_map/slice | solution.py:464
  46.8 23.5 %reduce_adam.1 = (f32[336,128]{1,0:T(8,128)}, f32[336,128]{1,0:T(8,128)}, f32[336,128]{1,0:T(8,128)}) custom-call(bf16[16,336,128]{2,1,0:T(8,128)(2,1)} %get-tuple-element.17.q_ref, f32[336,128]{1,0:T(8,128)} %bitcast.48, f32[336,128]{1,0:T(8,128)} %bitcast.47), custom_call_target="tpu_custom_call" | custom-call | tf_op jit(solution)/shard_map/reduce_adam/pallas_call | solution.py:351
  70.3 1.6 %copy.38 = f32[1,1,43008]{2,1,0:T(1,128)} copy(f32[1,1,43008]{2,1,0:T(1,128)} %bitcast.51) | data formatting | bytes 344064
  71.9 1.6 %copy.39 = f32[1,1,43008]{2,1,0:T(1,128)} copy(f32[1,1,43008]{2,1,0:T(1,128)} %bitcast.50) | data formatting | bytes 344064
  73.5 1.6 %copy.40 = f32[1,1,43008]{2,1,0:T(1,128)} copy(f32[1,1,43008]{2,1,0:T(1,128)} %bitcast.49) | data formatting | bytes 344064
  (3 shorter events, 0.0 us)
Async XLA Ops:
  0.6 0.8 %copy-start = (s32[1,8]{1,0:T(1,128)S(1)}, s32[1,8]{1,0:T(1,128)}, u32[]{:S(2)}) copy-start(s32[1,8]{1,0:T(1,128)} %param.15) | copy-start | bytes 100
  9.3 23.0 %copy-start.2 = (s32[1,16]{1,0:T(1,128)S(1)}, s32[1,16]{1,0:T(1,128)}, u32[]{:S(2)}) copy-start(s32[1,16]{1,0:T(1,128)} %param.16) | copy-start | bytes 196
  9.3 23.5 %copy-start.3 = (s32[8]{0:T(128)S(1)}, s32[8]{0:T(128)}, u32[]{:S(2)}) copy-start(s32[8]{0:T(128)} %param.17) | copy-start | bytes 100
  33.5 12.1 %copy-start.1 = (bf16[16,42,128]{2,1,0:T(8,128)(2,1)S(1)}, bf16[16,42,128]{2,1,0:T(8,128)(2,1)}, u32[]{:S(2)}) copy-start(bf16[16,42,128]{2,1,0:T(8,128)(2,1)} %get-tuple-element.18) | copy-start | bytes 516100

commit v2 on v1

--- a/solution.py
+++ b/solution.py
@@ -39,16 +39,21 @@
     pl.semaphore_wait(barrier, n - 1 + (extra is not None))
 
 
-def exchange_kernel(
-    n, x_hbm, l_hbm, win_ref, wout_ref, pieces_ref, pick_ref,
-    pre_ref, p_ref, w_ref, got_ref,
-    x_buf, l_buf, p_buf, spread, chosen,
+def relay_kernel(
+    n, block_rows, new_ref, old_ref, x_hbm, l_hbm, win_ref, wout_ref, m_ref, v_ref,
+    p_up_ref, w_ref, p_ref, total_ref, first_ref, second_ref,
+    order, x_buf, l_buf, p_buf, pieces, spread, chosen, got, gin, gout, turn,
+    blocks, outbox, near, summed, far,
     x_sem, l_sem, w_send, w_recv, f_send, f_recv, p_send, p_recv, a_send, a_recv, b_send, b_recv, own_sem,
+    s1, r1, s2, r2,
 ):
     me = lax.axis_index("dp")
-    other = 1 - lax.axis_index("section")
+    section = lax.axis_index("section")
+    other = 1 - section
     core = lax.rem(me, 2)
     sibling = me + 1 - 2 * core
+    chip = me // 2
+    chips = n // 2
     rank, width = win_ref.shape
     cw = column_width(width)
     chunks = width // cw
@@ -59,9 +64,23 @@
             load = pltpu.make_async_copy(src.at[:, cols], dst.at[:, cols], sem.at[c])
             load.start()
             loads.append(load)
-    own = pltpu.make_async_copy(pieces_ref.at[me], spread.at[me], own_sem.at[0])
-    own.start()
-    greet(n, me, other)
+    barrier = pltpu.get_barrier_semaphore()
+
+    @pl.loop(1, n)
+    def _(d):
+        pl.semaphore_signal(barrier, inc=1, device_id={"dp": lax.rem(me + d, n)}, device_id_type=MESH)
+
+    pl.semaphore_signal(barrier, inc=1, device_id={"section": other}, device_id_type=MESH)
+    part = block_rows // n
+    slab = pieces.shape[2] // 2
+    filler = [jnp.zeros((slab - part, 128), jnp.float32)] if slab > part else []
+    for t in range(n):
+        for h in range(2):
+            start = h * block_rows + t * part
+            pieces[t, h] = jnp.concatenate(
+                [m_ref[start : start + part, :]] + filler + [v_ref[start : start + part, :]] + filler, axis=0
+            ).astype(jnp.bfloat16)
+    pl.semaphore_wait(barrier, n)
     half = rank // 2
     mine = pl.ds(pl.multiple_of(core * half, half), half)
     theirs = pl.ds(pl.multiple_of((1 - core) * half, half), half)
@@ -73,34 +92,43 @@
     def spread_copy(d):
         peer = lax.rem(me + d, n)
         return pltpu.make_async_remote_copy(
-            pieces_ref.at[peer], spread.at[me], a_send.at[d], a_recv.at[d],
+            pieces.at[peer], spread.at[me], a_send.at[d], a_recv.at[d],
             device_id={"dp": peer}, device_id_type=MESH,
         )
 
     def spread_arrival(d):
         peer = lax.rem(me + n - d, n)
         return pltpu.make_async_remote_copy(
-            pieces_ref.at[peer], spread.at[peer], a_send.at[d], a_recv.at[d],
+            pieces.at[peer], spread.at[peer], a_send.at[d], a_recv.at[d],
             device_id={"dp": peer}, device_id_type=MESH,
         )
 
     def gather_copy(d):
         peer = lax.rem(me + d, n)
         return pltpu.make_async_remote_copy(
-            chosen.at[peer], got_ref.at[me], b_send.at[d], b_recv.at[d],
+            chosen.at[peer], got.at[me], b_send.at[d], b_recv.at[d],
             device_id={"dp": peer}, device_id_type=MESH,
         )
 
     def gather_arrival(d):
         peer = lax.rem(me + n - d, n)
         return pltpu.make_async_remote_copy(
-            chosen.at[peer], got_ref.at[peer], b_send.at[d], b_recv.at[d],
+            chosen.at[peer], got.at[peer], b_send.at[d], b_recv.at[d],
             device_id={"dp": peer}, device_id_type=MESH,
         )
 
     @pl.loop(1, n)
     def _(d):
         spread_copy(d).start()
+
+    own = pltpu.make_async_copy(pieces.at[me], spread.at[me], own_sem.at[0])
+    own.start()
+    owners = [new_ref[c] for c in range(n)]
+    for t in range(n):
+        block = jnp.int32(0)
+        for c in range(1, n):
+            block = jnp.where(owners[c] == t, c, block)
+        order[t] = block
 
     rows = x_buf.shape[0]
     pre = jnp.zeros((rows, rank), jnp.float32)
@@ -111,116 +139,200 @@
         loads[2 * c + 1].wait()
         pre = pre + nt_dot(x_buf[:, cols], win_ref[:, cols])
         act = act + nt_dot(l_buf[:, cols], wout_ref[:, cols])
-    pre_ref[...] = pre
-    p_buf[...] = (act * silu_slope(pre)).astype(jnp.bfloat16)
+    slope = silu_slope(pre)
+    p_buf[...] = (act * slope).astype(jnp.bfloat16)
     p_copy = pltpu.make_async_remote_copy(
-        p_buf, p_ref, p_send, p_recv, device_id={"section": other}, device_id_type=MESH
+        p_buf, p_up_ref, p_send, p_recv, device_id={"section": other}, device_id_type=MESH
     )
     p_copy.start()
-    own.wait()
-
-    @pl.loop(1, n)
-    def _(d):
-        spread_arrival(d).wait_recv()
-
-    for t in range(n):
-        chosen[t] = spread[pick_ref[t, 0], pick_ref[t, 1]]
-
-    @pl.loop(1, n)
-    def _(d):
-        gather_copy(d).start()
-
-    keep = pltpu.make_async_copy(chosen.at[me], got_ref.at[me], own_sem.at[1])
-    keep.start()
+    hidden_t = jax.nn.silu(pre).T.astype(jnp.bfloat16)
     w_copy.wait_recv()
     forward = pltpu.make_async_remote_copy(
         w_ref.at[mine], w_ref.at[mine], f_send, f_recv, device_id={"dp": sibling}, device_id_type=MESH
     )
     forward.start()
-    w_copy.wait_send()
-    p_copy.wait()
-    forward.wait_send()
     pltpu.make_async_remote_copy(
         w_ref.at[theirs], w_ref.at[theirs], f_send, f_recv, device_id={"dp": sibling}, device_id_type=MESH
     ).wait_recv()
+    p_copy.wait_recv()
+    p_in = jnp.where(section == 0, p_up_ref[...].astype(jnp.float32), 0.0).astype(jnp.bfloat16)
+    act = jnp.zeros((rows, rank), jnp.float32)
+    for c in range(chunks):
+        cols = pl.ds(c * cw, cw)
+        incoming = (
+            l_buf[:, cols].astype(jnp.float32)
+            + jnp.dot(p_in, w_ref[:, cols], preferred_element_type=jnp.float32)
+        ).astype(jnp.bfloat16)
+        act = act + nt_dot(incoming, wout_ref[:, cols])
+        gout[:, cols] = jnp.dot(hidden_t, incoming, preferred_element_type=jnp.float32)
+    grad = act * slope
+    p_ref[...] = grad.astype(jnp.bfloat16)
+    p_t = grad.T.astype(jnp.bfloat16)
+    own.wait()
+
+    @pl.loop(1, n)
+    def _(d):
+        spread_arrival(d).wait_recv()
+
+    for t in range(n):
+        block = order[t]
+        chosen[t] = spread[old_ref[block // 2], lax.rem(block, 2)]
+
+    @pl.loop(1, n)
+    def _(d):
+        gather_copy(d).start()
+
+    keep = pltpu.make_async_copy(chosen.at[me], got.at[me], own_sem.at[1])
+    keep.start()
+    for c in range(chunks):
+        cols = pl.ds(c * cw, cw)
+        gin[cols, :] = jnp.dot(p_t, x_buf[:, cols], preferred_element_type=jnp.float32).T
+    tiles = width // 128
+    lines = block_rows // tiles
+    for b in range(chips):
+        start = b * block_rows * 2
+        low = gin[pl.ds(start, block_rows, stride=2), :]
+        high = gin[pl.ds(start + 1, block_rows, stride=2), :]
+        blocks[b] = jnp.concatenate([low, high], axis=1).astype(jnp.bfloat16)
+    for b in range(chips):
+        for t in range(tiles):
+            turn[pl.ds(t, lines, stride=tiles), :] = gout[b * lines : (b + 1) * lines, t * 128 : (t + 1) * 128]
+        blocks[chips + b] = turn[...].astype(jnp.bfloat16)
+
+    def near_copy(d):
+        to = lax.rem(chip + d, chips)
+        return pltpu.make_async_remote_copy(
+            outbox.at[to], near.at[to], s1.at[d], r1.at[d], device_id={"dp": sibling}, device_id_type=MESH
+        )
+
+    def far_copy(d):
+        to = lax.rem(chip + d, chips)
+        return pltpu.make_async_remote_copy(
+            summed.at[to], far.at[d], s2.at[d], r2.at[d],
+            device_id={"dp": to * 2 + core}, device_id_type=MESH,
+        )
+
+    @pl.loop(1, chips + 1)
+    def _(step):
+        to = lax.rem(chip + step, chips)
+        outbox[to] = blocks[order[to * 2 + 1 - core]]
+        near_copy(lax.rem(step, chips)).start()
+
+    @pl.loop(1, chips)
+    def _(d):
+        to = lax.rem(chip + d, chips)
+        near_copy(d).wait_recv()
+        summed[to] = (
+            blocks[order[to * 2 + core]].astype(jnp.float32) + near[to].astype(jnp.float32)
+        ).astype(jnp.bfloat16)
+        far_copy(d).start()
+
+    near_copy(0).wait_recv()
+    total_ref[...] = blocks[order[me]].astype(jnp.float32) + near[chip].astype(jnp.float32)
     keep.wait()
+
+    @pl.loop(1, n)
+    def _(d):
+        gather_arrival(d).wait_recv()
+
+    for t in range(n):
+        place = pl.ds(t * part, part)
+        held = got[t].astype(jnp.float32)
+        first_ref[place, :] = held[:part, :]
+        second_ref[place, :] = held[slab : slab + part, :]
+
+    @pl.loop(1, chips)
+    def _(d):
+        far_copy(d).wait_recv()
+        total_ref[...] += far[d].astype(jnp.float32)
+
+    w_copy.wait_send()
+    p_copy.wait_send()
+    forward.wait_send()
 
     @pl.loop(1, n)
     def _(d):
         spread_copy(d).wait_send()
         gather_copy(d).wait_send()
-        gather_arrival(d).wait_recv()
-
-
-def exchange(n, x, loss, win, wout, pieces, picks):
+
+    @pl.loop(0, chips)
+    def _(d):
+        near_copy(d).wait_send()
+
+    @pl.loop(1, chips)
+    def _(d):
+        far_copy(d).wait_send()
+
+
+def relay(n, new_owner, old_owner, x, loss, win, wout, first, second):
     rows, width = x.shape
     rank = win.shape[0]
     chunks = width // column_width(width)
+    block_rows = first.shape[0] // 2
+    slab = -(-(block_rows // n) // 8) * 8
     dma = pltpu.SemaphoreType.DMA
+    bf16, f32 = jnp.bfloat16, jnp.float32
+    group = pltpu.VMEM((n // 2, block_rows, 128), bf16)
+    lines = jax.ShapeDtypeStruct((block_rows, 128), f32)
     return pl.pallas_call(
-        functools.partial(exchange_kernel, n),
+        functools.partial(relay_kernel, n, block_rows),
         out_shape=(
-            jax.ShapeDtypeStruct((rows, rank), jnp.float32),
-            jax.ShapeDtypeStruct((rows, rank), jnp.bfloat16),
-            jax.ShapeDtypeStruct((rank, width), jnp.bfloat16),
-            jax.ShapeDtypeStruct((n,) + pieces.shape[2:], jnp.bfloat16),
+            jax.ShapeDtypeStruct((rows, rank), bf16),
+            jax.ShapeDtypeStruct((rank, width), bf16),
+            jax.ShapeDtypeStruct((rows, rank), bf16),
+            lines, lines, lines,
         ),
-        in_specs=[ANY, ANY, VMEM, VMEM, VMEM, SMEM],
-        out_specs=(VMEM,) * 4,
+        in_specs=[SMEM, SMEM, ANY, ANY, VMEM, VMEM, VMEM, VMEM],
+        out_specs=(VMEM,) * 6,
         scratch_shapes=[
-            pltpu.VMEM(x.shape, jnp.bfloat16),
-            pltpu.VMEM(x.shape, jnp.bfloat16),
-            pltpu.VMEM((rows, rank), jnp.bfloat16),
-            pltpu.VMEM(pieces.shape, jnp.bfloat16),
-            pltpu.VMEM((n,) + pieces.shape[2:], jnp.bfloat16),
+            pltpu.SMEM((n,), jnp.int32),
+            pltpu.VMEM(x.shape, bf16),
+            pltpu.VMEM(x.shape, bf16),
+            pltpu.VMEM((rows, rank), bf16),
+            pltpu.VMEM((n, 2, 2 * slab, 128), bf16),
+            pltpu.VMEM((n, 2, 2 * slab, 128), bf16),
+            pltpu.VMEM((n, 2 * slab, 128), bf16),
+            pltpu.VMEM((n, 2 * slab, 128), bf16),
+            pltpu.VMEM((width, rank), f32),
+            pltpu.VMEM((rank, width), f32),
+            pltpu.VMEM((block_rows, 128), f32),
+            pltpu.VMEM((n, block_rows, 128), bf16),
+            group, group, group, group,
             dma((chunks,)), dma((chunks,)), dma, dma, dma, dma, dma, dma,
             dma((n,)), dma((n,)), dma((n,)), dma((n,)), dma((2,)),
+            dma((n // 2,)), dma((n // 2,)), dma((n // 2,)), dma((n // 2,)),
         ],
         compiler_params=pltpu.CompilerParams(collective_id=0, has_side_effects=True),
-        name="exchange",
-    )(x, loss, win, wout, pieces, picks)
-
-
-def drain_kernel(
-    n, relayed_ref, slot_ref, place_ref, x_hbm, l_hbm, pre_ref, p_in_ref, w_up_ref, win_ref, wout_ref,
-    out_hbm, q_ref,
-    x_buf, l_buf, o_buf, gin, gout, turn, x_sem, l_sem, o_sem,
+        name="relay",
+    )(new_owner, old_owner, x, loss, win, wout, first, second)
+
+
+def emit_kernel(
+    relayed_ref, slot_ref, l_hbm, p_up_ref, w_up_ref, p_ref, win_ref, total_ref, m_ref, v_ref,
+    out_hbm, u_ref, first_ref, second_ref,
+    l_buf, o_buf, l_sem, o_sem,
 ):
     rank, width = win_ref.shape
     micro_count, tok_rows, _ = out_hbm.shape
     cw = column_width(width)
     chunks = width // cw
-    loads_x, loads_l = [], []
+    loads = []
     for c in range(chunks):
         cols = pl.ds(c * cw, cw)
-        loads_l.append(pltpu.make_async_copy(l_hbm.at[:, cols], l_buf.at[:, cols], l_sem.at[c]))
-        loads_l[-1].start()
-    for c in range(chunks):
-        cols = pl.ds(c * cw, cw)
-        loads_x.append(pltpu.make_async_copy(x_hbm.at[:, cols], x_buf.at[:, cols], x_sem.at[c]))
-        loads_x[-1].start()
+        loads.append(pltpu.make_async_copy(l_hbm.at[:, cols], l_buf.at[:, cols], l_sem.at[c]))
+        loads[-1].start()
+    adam(total_ref[...], m_ref[...], v_ref[...], u_ref, first_ref, second_ref)
     is_relayed = relayed_ref[0] != 0
-    act = jnp.zeros((x_buf.shape[0], rank), jnp.float32)
-    p_in = jnp.where(is_relayed, p_in_ref[...].astype(jnp.float32), 0.0).astype(jnp.bfloat16)
-    for c in range(chunks):
-        cols = pl.ds(c * cw, cw)
-        loads_l[c].wait()
-        relayed = l_buf[:, cols].astype(jnp.float32) + jnp.dot(
-            p_in, w_up_ref[:, cols], preferred_element_type=jnp.float32
-        )
-        incoming = relayed.astype(jnp.bfloat16)
-        l_buf[:, cols] = incoming
-        act = act + nt_dot(incoming, wout_ref[:, cols])
-    pre = pre_ref[...]
-    hidden_t = jax.nn.silu(pre).T.astype(jnp.bfloat16)
-    grad = act * silu_slope(pre)
-    p_now = grad.astype(jnp.bfloat16)
-    p_t = grad.T.astype(jnp.bfloat16)
+    p_up = jnp.where(is_relayed, p_up_ref[...].astype(jnp.float32), 0.0).astype(jnp.bfloat16)
+    p_now = p_ref[...]
     stores = []
     for c in range(chunks):
         cols = pl.ds(c * cw, cw)
-        loads_x[c].wait()
-        incoming = l_buf[:, cols]
+        loads[c].wait()
+        incoming = (
+            l_buf[:, cols].astype(jnp.float32)
+            + jnp.dot(p_up, w_up_ref[:, cols], preferred_element_type=jnp.float32)
+        ).astype(jnp.bfloat16)
         o_buf[:, cols] = (
             incoming.astype(jnp.float32) + jnp.dot(p_now, win_ref[:, cols], preferred_element_type=jnp.float32)
         ).astype(jnp.bfloat16)
@@ -232,48 +344,43 @@
             )
             store.start()
             stores.append(store)
-        gin[cols, :] = jnp.dot(p_t, x_buf[:, cols], preferred_element_type=jnp.float32).T
-        gout[:, cols] = jnp.dot(hidden_t, incoming, preferred_element_type=jnp.float32)
-    block_rows = q_ref.shape[1]
-    tiles = width // 128
-    for b in range(n // 2):
-        start = b * block_rows * 2
-        low = gin[pl.ds(start, block_rows, stride=2), :]
-        high = gin[pl.ds(start + 1, block_rows, stride=2), :]
-        q_ref[place_ref[b]] = jnp.concatenate([low, high], axis=1).astype(jnp.bfloat16)
-    lines = block_rows // tiles
-    for b in range(n // 2):
-        for t in range(tiles):
-            turn[pl.ds(t, lines, stride=tiles), :] = gout[b * lines : (b + 1) * lines, t * 128 : (t + 1) * 128]
-        q_ref[place_ref[n // 2 + b]] = turn[...].astype(jnp.bfloat16)
     for store in stores:
         store.wait()
 
 
-def drain(n, block_len, micro_count, relayed, slots, places, x, loss, pre, p_in, w_up, win, wout):
-    rows, width = x.shape
-    rank = win.shape[0]
+def emit(micro_count, relayed, slots, loss, p_up, w_up, p_now, win, total, m, v):
+    rows, width = loss.shape
     chunks = width // column_width(width)
     dma = pltpu.SemaphoreType.DMA
+    lines = jax.ShapeDtypeStruct(m.shape, jnp.float32)
     return pl.pallas_call(
-        functools.partial(drain_kernel, n),
+        emit_kernel,
         out_shape=(
             jax.ShapeDtypeStruct((micro_count, rows // micro_count, width), jnp.bfloat16),
-            jax.ShapeDtypeStruct((n, block_len // 128, 128), jnp.bfloat16),
+            lines, lines, lines,
         ),
-        in_specs=[SMEM, SMEM, SMEM, ANY, ANY, VMEM, VMEM, VMEM, VMEM, VMEM],
-        out_specs=(ANY, VMEM),
+        in_specs=[SMEM, SMEM, ANY] + [VMEM] * 7,
+        out_specs=(ANY, VMEM, VMEM, VMEM),
         scratch_shapes=[
-            pltpu.VMEM(x.shape, jnp.bfloat16),
-            pltpu.VMEM(x.shape, jnp.bfloat16),
-            pltpu.VMEM(x.shape, jnp.bfloat16),
-            pltpu.VMEM((width, rank), jnp.float32),
-            pltpu.VMEM((rank, width), jnp.float32),
-            pltpu.VMEM((block_len // 128, 128), jnp.float32),
-            dma((chunks,)), dma((chunks,)), dma((chunks, micro_count)),
+            pltpu.VMEM(loss.shape, jnp.bfloat16),
+            pltpu.VMEM(loss.shape, jnp.bfloat16),
+            dma((chunks,)), dma((chunks, micro_count)),
         ],
-        name="drain",
-    )(relayed, slots, places, x, loss, pre, p_in, w_up, win, wout)
+        name="emit",
+    )(relayed, slots, loss, p_up, w_up, p_now, win, total, m, v)
+
+
+def adam(total, m, v, u_ref, first_ref, second_ref):
+    grads = total / loss_scale
+    first_next = beta_one * m + (1.0 - beta_one) * grads
+    second_next = beta_two * v + (1.0 - beta_two) * grads * grads
+    first_ref[...] = first_next
+    second_ref[...] = second_next
+    u_ref[...] = (
+        first_next
+        / (1.0 - beta_one**adam_step)
+        / (jnp.sqrt(second_next / (1.0 - beta_two**adam_step)) + adam_eps)
+    )
 
 
 def reduce_kernel(
@@ -323,16 +430,7 @@
         far_copy(d).wait_recv()
         first_ref[...] += far[d].astype(jnp.float32)
 
-    grads = first_ref[...] / loss_scale
-    first_next = beta_one * m_ref[...] + (1.0 - beta_one) * grads
-    second_next = beta_two * v_ref[...] + (1.0 - beta_two) * grads * grads
-    first_ref[...] = first_next
-    second_ref[...] = second_next
-    u_ref[...] = (
-        first_next
-        / (1.0 - beta_one**adam_step)
-        / (jnp.sqrt(second_next / (1.0 - beta_two**adam_step)) + adam_eps)
-    )
+    adam(first_ref[...], m_ref[...], v_ref[...], u_ref, first_ref, second_ref)
 
     @pl.loop(0, chips)
     def _(d):
@@ -435,34 +533,22 @@
     )
     place_of_block = owners_new % 2 * (replicas // 2) + owners_new // 2
     lines = (block_len // 128, 128)
-    if sections == 2:
+    if sections == 2 and replicas % 2 == 0 and block_len % (128 * replicas) == 0:
         rows = micro_count * tok_rows
         flat_inputs = inputs_all.reshape(rows, width)
         flat_loss = loss_grads.reshape(rows, width)
         turned_in = weight_in.T
-        piece_len = block_len // replicas
-        lanes = math.gcd(2 * piece_len, 128)
-        pieces = jnp.stack([first_moment[0, 0], second_moment[0, 0]]).astype(jnp.bfloat16)
-        pieces = pieces.reshape(2, 2, replicas, piece_len).transpose(2, 1, 0, 3)
-        pieces = pieces.reshape(replicas, 2, 2 * piece_len // lanes, lanes)
-        block_of = jnp.sum(
-            jnp.where(owners_new[None, :] == replica_ids[:, None], replica_ids[None, :], 0), axis=1
-        )
-        holder = owners_old[block_of // 2]
-        picks = jnp.stack([holder, block_of % 2], axis=1)
-        pre, p_up, w_up, got = exchange(
-            replicas, flat_inputs, flat_loss, turned_in, weight_out, pieces, picks
+        row_lines = (2 * block_len // 128, 128)
+        p_up, w_up, p_now, total, first_old, second_old = relay(
+            replicas, owners_new, owners_old, flat_inputs, flat_loss, turned_in, weight_out,
+            first_moment.reshape(row_lines), second_moment.reshape(row_lines),
         )
         slot_ids = jnp.arange(micro_count, dtype=jnp.int32)
         slots = jnp.sum(jnp.where(plan[None, :] == slot_ids[:, None], slot_ids[None, :], 0), axis=1)
         relayed = (section_index < sections - 1).astype(jnp.int32).reshape(1)
-        emitted, blocks = drain(
-            replicas, block_len, micro_count, relayed, slots, place_of_block,
-            flat_inputs, flat_loss, pre, p_up, w_up, turned_in, weight_out,
-        )
-        got = got.reshape(replicas, 2, piece_len).astype(jnp.float32)
-        first_old, second_old = (got[:, 0].reshape(lines), got[:, 1].reshape(lines))
-        update, first_next, second_next = reduce_adam(replicas, blocks, first_old, second_old)
+        emitted, update, first_next, second_next = emit(
+            micro_count, relayed, slots, flat_loss, p_up, w_up, p_now, turned_in, total, first_old, second_old
+        )
         shape = (1, 1, block_len)
         return (emitted[None], update.reshape(shape), first_next.reshape(shape), second_next.reshape(shape))
     last_grad, grad_in, grad_out, emitted = lax.fori_loop(

time: 75.5 us -> 53.3 us (0.71)
  the two profiles are of different devices: /device:TPU:15 before, /device:TPU:13 now
where the time goes in v2:
time: 53.3 us; the launch traced here: 53.1 us
  Pallas kernels  51.2 us (96%)
  other arithmetic  1.3 us (2%)
  between operations  0.65 us (1%)
    pallas_call x1, Pallas kernels, relay(): pl.pallas_call(functools.partial(relay_kernel, n, block_rows), out_shape=...  43.5 us
    pallas_call x1, Pallas kernels, emit(): pl.pallas_call(emit_kernel, out_shape=(jax.ShapeDtypeStruct((micro_count,...  7.69 us
    reduce_sum x1, other arithmetic, per_device(): jnp.sum(jnp.where(plan[None, :] == slot_ids[:, None], slot_ids[None, :],...  1.3 us

profile of v2, /device:TPU:13, one launch (start us, length us, event | category | flops | bytes accessed | tf_op | source)
XLA Modules:
  0.0 53.1 jit_solution(6017313198992495607)
XLA Ops:
  0.6 1.3 %select_reduce_fusion.slot_ref = s32[8]{0:T(128)} fusion(s32[8]{0:T(128)} %param.17), kind=kLoop, calls=%fused_computation | loop fusion | flops 184 | bytes 64 | tf_op jit(solution)/shard_map/reduce_sum | solution.py:547
  1.9 43.5 %relay.1 = (bf16[384,64]{1,0:T(8,128)(2,1)}, bf16[64,5376]{1,0:T(8,128)(2,1)}, bf16[384,64]{1,0:T(8,128)(2,1)}, f32[336,128]{1,0:T(8,128)}, f32[336,128]{1,0:T(8,128)}, /*index=5*/f32[336,128]{1,0:T(8,128)}) custom-call(s32[16]{0:T(128)} %bitcast.23, s32[8]{0:T(128)} %bitcast.24, bf16[384,5376]{1,0:T(8,128)(2,1)} %bitcast.17, bf16[384,5376]{1,0:T(8,128)(2,1)} %bitcast.15, ...), custom_call_target="tpu_custom_call" | custom-call | tf_op jit(solution)/shard_map/relay/pallas_call | solution.py:277
  45.5 7.7 %emit.1 = (bf16[8,48,5376]{2,1,0:T(8,128)(2,1)}, f32[336,128]{1,0:T(8,128)}, f32[336,128]{1,0:T(8,128)}, f32[336,128]{1,0:T(8,128)}) custom-call(s32[1]{0:T(128)} %bitcast.relayed_ref, s32[8]{0:T(128)} %select_reduce_fusion.slot_ref, bf16[384,5376]{1,0:T(8,128)(2,1)} %bitcast.16, bf16[384,64]{1,0:T(8,128)(2,1)} %get-tuple-element.14.p_up_ref, ...), custom_call_target="tpu_custom_call" | custom-call | tf_op jit(solution)/shard_map/emit/pallas_call | solution.py:356

commit v3 on v2

--- a/solution.py
+++ b/solution.py
@@ -43,9 +43,9 @@
     n, block_rows, new_ref, old_ref, x_hbm, l_hbm, win_ref, wout_ref, m_ref, v_ref,
     p_up_ref, w_ref, p_ref, total_ref, first_ref, second_ref,
     order, x_buf, l_buf, p_buf, pieces, spread, chosen, got, gin, gout, turn,
-    blocks, outbox, near, summed, far,
+    blocks, outbox, near, summed, mid, far,
     x_sem, l_sem, w_send, w_recv, f_send, f_recv, p_send, p_recv, a_send, a_recv, b_send, b_recv, own_sem,
-    s1, r1, s2, r2,
+    s1, r1, s2, r2, s3, r3,
 ):
     me = lax.axis_index("dp")
     section = lax.axis_index("section")
@@ -199,36 +199,64 @@
             turn[pl.ds(t, lines, stride=tiles), :] = gout[b * lines : (b + 1) * lines, t * 128 : (t + 1) * 128]
         blocks[chips + b] = turn[...].astype(jnp.bfloat16)
 
-    def near_copy(d):
-        to = lax.rem(chip + d, chips)
-        return pltpu.make_async_remote_copy(
-            outbox.at[to], near.at[to], s1.at[d], r1.at[d], device_id={"dp": sibling}, device_id_type=MESH
+    pairs = chips // 2
+    lane = lax.rem(chip, 2)
+    pair = chip // 2
+
+    def near_copy(to):
+        return pltpu.make_async_remote_copy(
+            outbox.at[to], near.at[to], s1.at[to], r1.at[to], device_id={"dp": sibling}, device_id_type=MESH
+        )
+
+    def mid_copy(at):
+        return pltpu.make_async_remote_copy(
+            summed.at[at * 2 + 1 - lane], mid.at[at], s3.at[at], r3.at[at],
+            device_id={"dp": (pair * 2 + 1 - lane) * 2 + core}, device_id_type=MESH,
         )
 
     def far_copy(d):
-        to = lax.rem(chip + d, chips)
+        to = lax.rem(pair + d, pairs) * 2 + lane
         return pltpu.make_async_remote_copy(
             summed.at[to], far.at[d], s2.at[d], r2.at[d],
             device_id={"dp": to * 2 + core}, device_id_type=MESH,
         )
 
-    @pl.loop(1, chips + 1)
+    for side in (1 - lane, lane):
+
+        @pl.loop(1, pairs + 1)
+        def _(step):
+            to = lax.rem(pair + step, pairs) * 2 + side
+            outbox[to] = blocks[order[to * 2 + 1 - core]]
+            near_copy(to).start()
+
+    @pl.loop(1, pairs + 1)
     def _(step):
-        to = lax.rem(chip + step, chips)
-        outbox[to] = blocks[order[to * 2 + 1 - core]]
-        near_copy(lax.rem(step, chips)).start()
-
-    @pl.loop(1, chips)
-    def _(d):
-        to = lax.rem(chip + d, chips)
-        near_copy(d).wait_recv()
+        at = lax.rem(pair + step, pairs)
+        to = at * 2 + 1 - lane
+        near_copy(to).wait_recv()
         summed[to] = (
             blocks[order[to * 2 + core]].astype(jnp.float32) + near[to].astype(jnp.float32)
         ).astype(jnp.bfloat16)
+        mid_copy(at).start()
+
+    @pl.loop(1, pairs)
+    def _(d):
+        at = lax.rem(pair + d, pairs)
+        to = at * 2 + lane
+        near_copy(to).wait_recv()
+        mid_copy(at).wait_recv()
+        summed[to] = (
+            blocks[order[to * 2 + core]].astype(jnp.float32)
+            + near[to].astype(jnp.float32)
+            + mid[at].astype(jnp.float32)
+        ).astype(jnp.bfloat16)
         far_copy(d).start()
 
-    near_copy(0).wait_recv()
-    total_ref[...] = blocks[order[me]].astype(jnp.float32) + near[chip].astype(jnp.float32)
+    near_copy(chip).wait_recv()
+    mid_copy(pair).wait_recv()
+    total_ref[...] = (
+        blocks[order[me]].astype(jnp.float32) + near[chip].astype(jnp.float32) + mid[pair].astype(jnp.float32)
+    )
     keep.wait()
 
     @pl.loop(1, n)
@@ -241,7 +269,7 @@
         first_ref[place, :] = held[:part, :]
         second_ref[place, :] = held[slab : slab + part, :]
 
-    @pl.loop(1, chips)
+    @pl.loop(1, pairs)
     def _(d):
         far_copy(d).wait_recv()
         total_ref[...] += far[d].astype(jnp.float32)
@@ -259,7 +287,11 @@
     def _(d):
         near_copy(d).wait_send()
 
-    @pl.loop(1, chips)
+    @pl.loop(0, pairs)
+    def _(d):
+        mid_copy(d).wait_send()
+
+    @pl.loop(1, pairs)
     def _(d):
         far_copy(d).wait_send()
 
@@ -273,6 +305,7 @@
     dma = pltpu.SemaphoreType.DMA
     bf16, f32 = jnp.bfloat16, jnp.float32
     group = pltpu.VMEM((n // 2, block_rows, 128), bf16)
+    fewer = pltpu.VMEM((n // 4, block_rows, 128), bf16)
     lines = jax.ShapeDtypeStruct((block_rows, 128), f32)
     return pl.pallas_call(
         functools.partial(relay_kernel, n, block_rows),
@@ -297,10 +330,10 @@
             pltpu.VMEM((rank, width), f32),
             pltpu.VMEM((block_rows, 128), f32),
             pltpu.VMEM((n, block_rows, 128), bf16),
-            group, group, group, group,
+            group, group, group, fewer, fewer,
             dma((chunks,)), dma((chunks,)), dma, dma, dma, dma, dma, dma,
             dma((n,)), dma((n,)), dma((n,)), dma((n,)), dma((2,)),
-            dma((n // 2,)), dma((n // 2,)), dma((n // 2,)), dma((n // 2,)),
+            dma((n // 2,)), dma((n // 2,)), dma((n // 4,)), dma((n // 4,)), dma((n // 4,)), dma((n // 4,)),
         ],
         compiler_params=pltpu.CompilerParams(collective_id=0, has_side_effects=True),
         name="relay",
@@ -308,7 +341,7 @@
 
 
 def emit_kernel(
-    relayed_ref, slot_ref, l_hbm, p_up_ref, w_up_ref, p_ref, win_ref, total_ref, m_ref, v_ref,
+    plan_ref, l_hbm, p_up_ref, w_up_ref, p_ref, win_ref, total_ref, m_ref, v_ref,
     out_hbm, u_ref, first_ref, second_ref,
     l_buf, o_buf, l_sem, o_sem,
 ):
@@ -322,7 +355,7 @@
         loads.append(pltpu.make_async_copy(l_hbm.at[:, cols], l_buf.at[:, cols], l_sem.at[c]))
         loads[-1].start()
     adam(total_ref[...], m_ref[...], v_ref[...], u_ref, first_ref, second_ref)
-    is_relayed = relayed_ref[0] != 0
+    is_relayed = lax.axis_index("section") == 0
     p_up = jnp.where(is_relayed, p_up_ref[...].astype(jnp.float32), 0.0).astype(jnp.bfloat16)
     p_now = p_ref[...]
     stores = []
@@ -338,8 +371,8 @@
         ).astype(jnp.bfloat16)
         for m in range(micro_count):
             store = pltpu.make_async_copy(
-                o_buf.at[pl.ds(m * tok_rows, tok_rows), cols],
-                out_hbm.at[slot_ref[m], :, cols],
+                o_buf.at[pl.ds(pl.multiple_of(plan_ref[m] * tok_rows, tok_rows), tok_rows), cols],
+                out_hbm.at[m, :, cols],
                 o_sem.at[c, m],
             )
             store.start()
@@ -348,7 +381,7 @@
         store.wait()
 
 
-def emit(micro_count, relayed, slots, loss, p_up, w_up, p_now, win, total, m, v):
+def emit(micro_count, plan, loss, p_up, w_up, p_now, win, total, m, v):
     rows, width = loss.shape
     chunks = width // column_width(width)
     dma = pltpu.SemaphoreType.DMA
@@ -359,7 +392,7 @@
             jax.ShapeDtypeStruct((micro_count, rows // micro_count, width), jnp.bfloat16),
             lines, lines, lines,
         ),
-        in_specs=[SMEM, SMEM, ANY] + [VMEM] * 7,
+        in_specs=[SMEM, ANY] + [VMEM] * 7,
         out_specs=(ANY, VMEM, VMEM, VMEM),
         scratch_shapes=[
             pltpu.VMEM(loss.shape, jnp.bfloat16),
@@ -367,7 +400,7 @@
             dma((chunks,)), dma((chunks, micro_count)),
         ],
         name="emit",
-    )(relayed, slots, loss, p_up, w_up, p_now, win, total, m, v)
+    )(plan, loss, p_up, w_up, p_now, win, total, m, v)
 
 
 def adam(total, m, v, u_ref, first_ref, second_ref):
@@ -533,7 +566,7 @@
     )
     place_of_block = owners_new % 2 * (replicas // 2) + owners_new // 2
     lines = (block_len // 128, 128)
-    if sections == 2 and replicas % 2 == 0 and block_len % (128 * replicas) == 0:
+    if sections == 2 and replicas % 4 == 0 and block_len % (128 * replicas) == 0:
         rows = micro_count * tok_rows
         flat_inputs = inputs_all.reshape(rows, width)
         flat_loss = loss_grads.reshape(rows, width)
@@ -543,11 +576,8 @@
             replicas, owners_new, owners_old, flat_inputs, flat_loss, turned_in, weight_out,
             first_moment.reshape(row_lines), second_moment.reshape(row_lines),
         )
-        slot_ids = jnp.arange(micro_count, dtype=jnp.int32)
-        slots = jnp.sum(jnp.where(plan[None, :] == slot_ids[:, None], slot_ids[None, :], 0), axis=1)
-        relayed = (section_index < sections - 1).astype(jnp.int32).reshape(1)
         emitted, update, first_next, second_next = emit(
-            micro_count, relayed, slots, flat_loss, p_up, w_up, p_now, turned_in, total, first_old, second_old
+            micro_count, plan, flat_loss, p_up, w_up, p_now, turned_in, total, first_old, second_old
         )
         shape = (1, 1, block_len)
         return (emitted[None], update.reshape(shape), first_next.reshape(shape), second_next.reshape(shape))

time: 53.3 us -> 49.2 us (0.923)
  the two profiles are of different devices: /device:TPU:13 before, /device:TPU:0 now
where the time goes in v3:
time: 49.2 us; the launch traced here: 49 us
  Pallas kernels  48.4 us (98%)
  between operations  0.64 us (1%)
    pallas_call x1, Pallas kernels, relay(): pl.pallas_call(functools.partial(relay_kernel, n, block_rows), out_shape=...  40.7 us
    pallas_call x1, Pallas kernels, emit(): pl.pallas_call(emit_kernel, out_shape=(jax.ShapeDtypeStruct((micro_count,...  7.68 us

profile of v3, /device:TPU:0, one launch (start us, length us, event | category | flops | bytes accessed | tf_op | source)
XLA Modules:
  0.0 49.0 jit_solution(10999001920644191439)
XLA Ops:
  0.6 40.7 %relay.1 = (bf16[384,64]{1,0:T(8,128)(2,1)}, bf16[64,5376]{1,0:T(8,128)(2,1)}, bf16[384,64]{1,0:T(8,128)(2,1)}, f32[336,128]{1,0:T(8,128)}, f32[336,128]{1,0:T(8,128)}, /*index=5*/f32[336,128]{1,0:T(8,128)}) custom-call(s32[16]{0:T(128)} %bitcast.22, s32[8]{0:T(128)} %bitcast.23, bf16[384,5376]{1,0:T(8,128)(2,1)} %bitcast.16, bf16[384,5376]{1,0:T(8,128)(2,1)} %bitcast.14, ...), custom_call_target="tpu_custom_call" | custom-call | tf_op jit(solution)/shard_map/relay/pallas_call | solution.py:310
  41.4 7.7 %emit.1 = (bf16[8,48,5376]{2,1,0:T(8,128)(2,1)}, f32[336,128]{1,0:T(8,128)}, f32[336,128]{1,0:T(8,128)}, f32[336,128]{1,0:T(8,128)}) custom-call(s32[8]{0:T(128)} %plan_ref.1, bf16[384,5376]{1,0:T(8,128)(2,1)} %bitcast.15, bf16[384,64]{1,0:T(8,128)(2,1)} %get-tuple-element.14.p_up_ref, bf16[64,5376]{1,0:T(8,128)(2,1)} %get-tuple-element.15.w_up_ref, ...), custom_call_target="tpu_custom_call" | custom-call | tf_op jit(solution)/shard_map/emit/pallas_call | solution.py:389
